TPU v7x, 32 devices: a whole 2x2x4 slice. The times are simulated.
32 devices in a mesh: seq: 8 (over z, y), head: 4 (over x, core).
Axes of the slice: x: 2, y: 2, z: 4, core: 2. Of those that a mesh axis runs over, the one named last changes fastest.
Arguments:
- q_low: bfloat16 [2048, 1536], P('seq', 'head'), may hold values from -500 to 500
- q_gain: bfloat16 [1536], P('head'), may hold values from 0.099609375 to 1.8984375
- q_up: bfloat16 [1536, 24576], P(None, 'head'), may hold values from -0.15625 to 0.15625
- key_absorb: bfloat16 [128, 128, 512], P('head'), may hold values from -0.5 to 0.5
- value_absorb: bfloat16 [128, 512, 128], P('head'), may hold values from -0.25 to 0.25
- latent_cache: bfloat16 [65536, 576], P('seq'), may hold values from -1300 to 1300
- tile_picks: int32 [16, 16], P('seq'), may hold values from 0 to 511, as said below
Outputs:
- attended: bfloat16 [2048, 16384], P('seq', 'head')
Inputs may be any that keep to these rules, and one draw needn't show every extreme that they name: `tile_picks`: the 16 tiles of one query block differ. Of all tiles that the query blocks of one index of seq select together, at most 8 lie in the cache rows of one index of seq, and exactly 8 in those of some index.
All inputs are finite; a program needn't handle non-finite values.
Results may differ from a plain program's by a relative error of at most 0.03.
Values may be sent and summed in bfloat16 or wider, within the bound.
A program may use at most 192 MiB of HBM per device.

v0:
```python
import jax
import jax.numpy as jnp
from jax import lax
from jax.experimental import pallas as pl
from jax.experimental.pallas import tpu as pltpu
from jax.sharding import PartitionSpec as P

NOPE = 128
ROPE = 64
LATENT = 512
VDIM = 128
TILE = 128
TOPT = 16
QBLK = 128
LANES = 128
LOG2E = 1.4426950408889634


def rms_normed(q_low, q_gain):
    values = q_low.astype(jnp.float32)
    power = jnp.mean(values * values, axis=-1, keepdims=True)
    return (values * lax.rsqrt(power + 1e-06) * q_gain.astype(jnp.float32)).astype(jnp.bfloat16)


def rotary_tables(positions):
    half = ROPE // 2
    freq = jnp.power(
        jnp.float32(10000.0), -(2.0 * jnp.arange(half, dtype=jnp.float32)) / ROPE
    )
    angle = positions.astype(jnp.float32)[:, None] * freq[None, :]
    cosine, sine = jnp.cos(angle), jnp.sin(angle)
    return (
        jnp.concatenate([cosine, cosine], axis=-1),
        jnp.concatenate([-sine, sine], axis=-1),
    )


def absorb_kernel(query_ref, absorb_ref, cos_ref, sin_ref, out_ref):
    heads = absorb_ref.shape[0]
    rows = query_ref.shape[0]
    half = ROPE // 2
    cosine, sine = cos_ref[...], sin_ref[...]
    for head in range(heads):
        start = head * (NOPE + ROPE)
        nope = query_ref[:, start : start + NOPE]
        rope = query_ref[:, start + NOPE : start + NOPE + ROPE].astype(jnp.float32)
        swapped = jnp.concatenate([rope[:, half:], rope[:, :half]], axis=-1)
        rotated = rope * cosine + swapped * sine
        out_ref[head, :, :LATENT] = jnp.dot(
            nope, absorb_ref[head], preferred_element_type=jnp.float32
        ).astype(jnp.bfloat16)
        out_ref[head, :, LATENT:] = jnp.concatenate(
            [rotated, jnp.zeros((rows, LANES - ROPE), jnp.float32)], axis=-1
        ).astype(jnp.bfloat16)


def absorbed_query(query, key_absorb, cosine, sine):
    rows = query.shape[0]
    group = key_absorb.shape[0]
    step = min(8, group)
    width = LATENT + LANES
    return pl.pallas_call(
        absorb_kernel,
        grid=(group // step,),
        in_specs=[
            pl.BlockSpec((rows, step * (NOPE + ROPE)), lambda i: (0, i)),
            pl.BlockSpec((step, NOPE, LATENT), lambda i: (i, 0, 0)),
            pl.BlockSpec((rows, ROPE), lambda i: (0, 0)),
            pl.BlockSpec((rows, ROPE), lambda i: (0, 0)),
        ],
        out_specs=pl.BlockSpec((step, rows, width), lambda i: (i, 0, 0)),
        out_shape=jax.ShapeDtypeStruct((group, rows, width), jnp.bfloat16),
        cost_estimate=pl.CostEstimate(
            flops=2 * rows * group * NOPE * LATENT,
            bytes_accessed=2 * (query.size + key_absorb.size + group * rows * width),
            transcendentals=0,
        ),
        name="absorb",
    )(query, key_absorb, cosine, sine)


def attend_kernel(query_ref, keys_ref, absorb_ref, out_ref, turned, values):
    heads = absorb_ref.shape[0]
    tiles, width = keys_ref.shape[1:3]

    @pl.when(pl.program_id(1) == 0)
    def _():
        turned[width:, :] = jnp.zeros((turned.shape[0] - width, turned.shape[1]), turned.dtype)
        for tile in range(tiles):
            span = slice(tile * TILE, (tile + 1) * TILE)
            turned[:width, span] = keys_ref[0, tile]
            values[span, :] = keys_ref[0, tile, :LATENT, :].T

    scale = float(NOPE + ROPE) ** (-0.5) * LOG2E
    pair = 2
    scores = []
    for at in range(0, heads, pair):
        block = query_ref[at : at + pair].reshape(pair * QBLK, query_ref.shape[2])
        scores.append(
            jnp.dot(block, turned[...], preferred_element_type=jnp.float32)
        )
    for at in range(0, heads, pair):
        score = scores[at // pair]
        top = jnp.max(score, axis=-1, keepdims=True)
        weights = jnp.exp2((score - top) * scale)
        total = jnp.sum(weights, axis=-1, keepdims=True)
        mixed = jnp.dot(
            weights.astype(jnp.bfloat16),
            values[...],
            preferred_element_type=jnp.float32,
        )
        mixed = (mixed / total).astype(jnp.bfloat16)
        for head in range(pair):
            out_ref[:, (at + head) * VDIM : (at + head + 1) * VDIM] = jnp.dot(
                mixed[head * QBLK : (head + 1) * QBLK],
                absorb_ref[at + head],
                preferred_element_type=jnp.float32,
            ).astype(jnp.bfloat16)


def attend(full_q, keys, value_absorb):
    group, rows, padded = full_q.shape
    blocks, tiles, width = keys.shape[:3]
    count = tiles * TILE
    step = min(4, group)
    return pl.pallas_call(
        attend_kernel,
        grid=(blocks, group // step),
        in_specs=[
            pl.BlockSpec((step, QBLK, padded), lambda b, g: (g, b, 0)),
            pl.BlockSpec((1, tiles, width, TILE), lambda b, g: (b, 0, 0, 0)),
            pl.BlockSpec((step, LATENT, VDIM), lambda b, g: (g, 0, 0)),
        ],
        out_specs=pl.BlockSpec((QBLK, step * VDIM), lambda b, g: (b, g)),
        out_shape=jax.ShapeDtypeStruct((rows, group * VDIM), jnp.bfloat16),
        scratch_shapes=[
            pltpu.VMEM((padded, count), jnp.bfloat16),
            pltpu.VMEM((count, LATENT), jnp.bfloat16),
        ],
        compiler_params=pltpu.CompilerParams(
            dimension_semantics=("arbitrary", "arbitrary"), vmem_limit_bytes=60 * 1024 * 1024
        ),
        cost_estimate=pl.CostEstimate(
            flops=2 * rows * group * count * (padded + LATENT),
            bytes_accessed=2 * (full_q.size + keys.size + value_absorb.size * blocks),
            transcendentals=rows * group * count,
        ),
        name="attend",
    )(full_q, keys, value_absorb)


def owner_rank(picks, tiles_dev):
    owner = picks // tiles_dev
    order = jnp.arange(picks.shape[0], dtype=jnp.int32)
    same = picks[:, None] == picks[None, :]
    first = jnp.min(jnp.where(same, order[None, :], picks.shape[0]), axis=1)
    fresh = first == order
    before = (owner[:, None] == owner[None, :]) & fresh[None, :] & (order[None, :] < first[:, None])
    return (owner, jnp.sum(before.astype(jnp.int32), axis=1), fresh)


def place_table(place, local, length):
    hit = place[:, None] == jnp.arange(length, dtype=jnp.int32)[None, :]
    return jnp.sum(jnp.where(hit, local[:, None], 0), axis=0)


def body(q_low, q_gain, q_up, key_absorb, value_absorb, latent_cache, tile_picks):
    whole_low, whole_gain = (
        lax.all_gather(q_low, "head", axis=1, tiled=True),
        lax.all_gather(q_gain, "head", axis=0, tiled=True),
    )
    rows = whole_low.shape[0]
    width = latent_cache.shape[1]
    seq_count = lax.axis_size("seq")
    tiles_dev = latent_cache.shape[0] // TILE
    picks = tile_picks.reshape(-1)
    count = picks.shape[0]
    cap = max(2, 2 * count // seq_count)
    owner, rank, fresh = owner_rank(picks, tiles_dev)
    share = width // lax.axis_size("head")
    columns = lax.dynamic_slice_in_dim(latent_cache, lax.axis_index("head") * share, share, 1)
    cache_tiles = columns.T.reshape(share, tiles_dev, TILE).transpose(1, 0, 2)
    requests = place_table(
        owner * cap + rank, jnp.where(fresh, picks % tiles_dev, 0), seq_count * cap
    ).reshape(
        seq_count, cap
    )
    serve_requests = lax.all_to_all(requests, "seq", split_axis=0, concat_axis=0, tiled=True)
    found = jnp.take(cache_tiles, serve_requests, axis=0, mode="clip")
    fetched = lax.all_to_all(found, "seq", split_axis=0, concat_axis=0, tiled=True)
    flat = fetched.reshape(seq_count * cap, share, TILE)
    keys = jnp.take(flat, owner * cap + rank, axis=0, mode="clip")
    normed = rms_normed(whole_low, whole_gain)
    query = jnp.dot(normed, q_up, preferred_element_type=jnp.float32).astype(jnp.bfloat16)
    keys, query = lax.optimization_barrier((keys, query))
    keys = lax.all_gather(keys, "head", axis=1, tiled=True)
    keys = keys.reshape(count // TOPT, TOPT, width, TILE)
    context = latent_cache.shape[0] * seq_count
    positions = context + lax.axis_index("seq") * rows + jnp.arange(rows, dtype=jnp.int32)
    full_q = absorbed_query(query, key_absorb, *rotary_tables(positions))
    return attend(full_q, keys, value_absorb)


def solution(mesh):
    in_specs = (
        P("seq", "head"),
        P("head"),
        P(None, "head"),
        P("head", None, None),
        P("head", None, None),
        P("seq", None),
        P("seq", None),
    )
    out_specs = P("seq", "head")
    return jax.shard_map(body, mesh=mesh, in_specs=in_specs, out_specs=out_specs, check_vma=False)
```

profile of v0, /device:TPU:0, one launch (start us, length us, event | category | flops | bytes accessed | tf_op | source)
XLA Modules:
  0.0 188.6 jit_solution(5399454564548222869)
XLA Ops:
  6.5 0.8 reshape.199
  7.3 0.2 select_reduce_fusion.1
  7.5 0.2 convert_reduce_fusion
  7.7 0.1 select_reduce_fusion
  7.8 0.7 all_to_all.9
  8.5 7.3 %all-to-all-start = ((s32[8,1,8]{2,1,0:T(1,128)}), s32[8,1,8]{2,1,0:T(1,128)S(1)}, u32[]{:S(2)}, u32[]{:S(2)}) async-start(s32[8,1,8]{2,1,0:T(1,128)} %bitcast.2), calls=%async_computation | async-start | bytes 8192 | tf_op jit(solution)/shard_map/all_to_all | solution.py:188
  15.8 2.1 %bitcast_bitcast_fusion = bf16[64,144,128]{2,1,0:T(8,128)(2,1)S(1)} fusion(bf16[8192,576]{0,1:T(8,128)(2,1)} %param.12, s32[]{:T(128)S(6)} %select_n.52), kind=kLoop, calls=%fused_computation.3 | loop fusion | bytes 4718596 | tf_op jit(solution)/shard_map/transpose | solution.py:182
  17.9 4.3 %all-to-all-done = s32[8,1,8]{2,1,0:T(1,128)S(1)} async-done(((s32[8,1,8]{2,1,0:T(1,128)}), s32[8,1,8]{2,1,0:T(1,128)S(1)}, u32[]{:S(2)}, u32[]{:S(2)}) %all-to-all-start) | async-done | bytes 288 | tf_op jit(solution)/shard_map/all_to_all | solution.py:188
  22.2 0.5 broadcast.203
  22.7 0.7 reduce.5
  23.4 0.1 reshape.205
  23.5 2.3 %gather_fusion = bf16[64,144,128]{2,1,0:T(8,128)(2,1)} fusion(bf16[64,144,128]{2,1,0:T(8,128)(2,1)S(1)} %bitcast_bitcast_fusion, s32[1024]{0:T(1024)S(1)} %pad_clamp_fusion.1), kind=kCustom, calls=%fused_computation | custom fusion | bytes 4718848 | tf_op jit(solution)/shard_map/jit(_take)/gather | solution.py:189
  25.7 0.0 copy-start.2
  25.7 0.0 copy-start.1
  25.7 0.0 copy-start
  25.7 3.7 %all-to-all-start.1 = ((bf16[8,8,144,128]{3,2,1,0:T(8,128)(2,1)}), bf16[8,8,144,128]{3,2,1,0:T(8,128)(2,1)S(1)}, u32[]{:S(2)}, u32[]{:S(2)}) async-start(bf16[8,8,144,128]{3,2,1,0:T(8,128)(2,1)} %bitcast.3), calls=%async_computation.1 | async-start | bytes 4718592 | tf_op jit(solution)/shard_map/all_to_all | solution.py:190
  29.5 0.0 all-gather.3.cloned.1.call-start
  29.5 0.0 copy-done.2
  29.6 0.1 reshape.201
  29.6 0.0 copy-done.1
  29.6 5.2 %all-gather = bf16[4,1,384]{2,1,0:T(2,128)(2,1)S(1)} all-gather(bf16[1,1,384]{2,1,0:T(2,128)(2,1)S(1)} %reshape.221), channel_id=1, replica_groups=mesh['seq'=8,'head'=4] {'head'}, dimensions={0}, use_global_device_ids=true | all-gather | bytes 3840 | tf_op jit(solution)/shard_map/all_gather | solution.py:170
  34.9 0.0 copy-done
  34.9 8.7 %all_gather.9 = bf16[256,1536]{1,0:T(8,128)(2,1)S(1)} all-gather(bf16[256,384]{1,0:T(8,128)(2,1)S(1)} %copy-done), channel_id=1, replica_groups=mesh['seq'=8,'head'=4] {'head'}, dimensions={1}, use_global_device_ids=true | all-gather | bytes 983040 | tf_op jit(solution)/shard_map/all_gather | solution.py:169
  43.6 0.2 fusion
  43.8 13.0 %convolution_convert_fusion.query_ref = bf16[256,6144]{1,0:T(8,128)(2,1)} fusion(bf16[1536,6144]{1,0:T(8,128)(2,1)} %param.9, bf16[256,1536]{1,0:T(8,128)(2,1)S(1)} %all_gather.9, f32[1536]{0:T(1024)S(1)} %reshape.223, f32[256]{0:T(256)S(1)} %add_rsqrt_fusion), kind=kOutput, calls=%fused_computation.2 | convolution fusion | flops 4834983936 | bytes 22813696 | tf_op jit(solution)/shard_map/dot_general | solution.py:194
  56.9 25.3 %all-to-all-done.1 = bf16[8,8,144,128]{3,2,1,0:T(8,128)(2,1)S(1)} async-done(((bf16[8,8,144,128]{3,2,1,0:T(8,128)(2,1)}), bf16[8,8,144,128]{3,2,1,0:T(8,128)(2,1)S(1)}, u32[]{:S(2)}, u32[]{:S(2)}) %all-to-all-start.1) | async-done | bytes 2359328 | tf_op jit(solution)/shard_map/all_to_all | solution.py:190
  82.1 1.7 gather_fusion.1
  83.8 0.0 all-gather.3.cloned.1.call-update
  83.9 0.5 fusion.6
  84.4 0.9 pad_maximum_fusion
  85.3 9.8 %absorb.1.query_ref = bf16[32,256,640]{2,1,0:T(8,128)(2,1)} custom-call(bf16[256,6144]{1,0:T(8,128)(2,1)} %convolution_convert_fusion.query_ref, bf16[32,128,512]{2,1,0:T(8,128)(2,1)} %absorb_ref.2, f32[256,64]{1,0:T(8,128)} %get-tuple-element.14.cos_ref, f32[256,64]{1,0:T(8,128)} %get-tuple-element.15.sin_ref), custom_call_target="tpu_custom_call" | custom-call | flops 1073741824 | bytes 17825792 | tf_op jit(solution)/shard_map/absorb/pallas_call | solution.py:62
  95.1 25.4 %all-gather.3.cloned.1.call-done = bf16[32,576,128]{2,1,0:T(8,128)(2,1)} async-done(((bf16[32,144,128]{2,1,0:T(8,128)(2,1)}), bf16[32,576,128]{2,1,0:T(8,128)(2,1)}) %all-gather.3.cloned.1.call-update) | async-done | bytes 4718608 | tf_op jit(solution)/shard_map/all_gather | solution.py:196
  120.5 61.2 %attend.1 = bf16[256,4096]{1,0:T(8,128)(2,1)} custom-call(bf16[32,256,640]{2,1,0:T(8,128)(2,1)} %absorb.1.query_ref, bf16[2,16,576,128]{3,2,1,0:T(8,128)(2,1)} %bitcast.20, bf16[32,512,128]{2,1,0:T(8,128)(2,1)} %absorb_ref.3), custom_call_target="tpu_custom_call" | custom-call | flops 38654705664 | bytes 23592960 | tf_op jit(solution)/shard_map/attend/pallas_call | solution.py:126
  (12 shorter events, 0.1 us)
Async XLA Ops:
  8.5 13.7 %all-to-all-start = ((s32[8,1,8]{2,1,0:T(1,128)}), s32[8,1,8]{2,1,0:T(1,128)S(1)}, u32[]{:S(2)}, u32[]{:S(2)}) async-start(s32[8,1,8]{2,1,0:T(1,128)} %bitcast.2), calls=%async_computation | async-start | bytes 8192 | tf_op jit(solution)/shard_map/all_to_all | solution.py:188
  25.7 3.8 %copy-start.2 = (s32[2,16]{1,0:T(2,128)S(1)}, s32[2,16]{1,0:T(2,128)}, u32[]{:S(2)}) copy-start(s32[2,16]{1,0:T(2,128)} %param.13) | copy-start | bytes 388
  25.7 3.9 %copy-start.1 = (bf16[384]{0:T(512)(128)(2,1)S(1)}, bf16[384]{0:T(512)(128)(2,1)}, u32[]{:S(2)}) copy-start(bf16[384]{0:T(512)(128)(2,1)} %param.8) | copy-start | bytes 2308
  25.7 9.1 %copy-start = (bf16[256,384]{1,0:T(8,128)(2,1)S(1)}, bf16[256,384]{1,0:T(8,128)(2,1)}, u32[]{:S(2)}) copy-start(bf16[256,384]{1,0:T(8,128)(2,1)} %param.7) | copy-start | bytes 589828
  25.7 56.4 %all-to-all-start.1 = ((bf16[8,8,144,128]{3,2,1,0:T(8,128)(2,1)}), bf16[8,8,144,128]{3,2,1,0:T(8,128)(2,1)S(1)}, u32[]{:S(2)}, u32[]{:S(2)}) async-start(bf16[8,8,144,128]{3,2,1,0:T(8,128)(2,1)} %bitcast.3), calls=%async_computation.1 | async-start | bytes 4718592 | tf_op jit(solution)/shard_map/all_to_all | solution.py:190
  29.5 91.0 %all-gather.3.cloned.1.call-start = ((), (), s32[]{:S(2)}) async-start(), calls=%async_computation.2 | async-start | bytes 5898240 | tf_op jit(solution)/shard_map/all_gather | solution.py:196
Sparse Core Ops, SparseCore 0:
  84.0 36.4 all-gather.2
where the time goes:
time: 189 us
  Pallas kernels  71 us (38%)
  waiting for transfers between devices  55.1 us (29%)
  blocking collectives  13.9 us (7%)
  between operations  13.5 us (7%)
  matrix products  13 us (7%)
  starting transfers between devices  11.1 us (6%)
  local copies, waits for them, and re-layouts  8.19 us (4%)
  other arithmetic  2.84 us (2%)
    pallas_call x1, Pallas kernels, attend(): pl.pallas_call(attend_kernel, grid=(blocks, group // step), in_specs=[pl....  61.2 us
    all_gather x1, waiting for transfers between devices, body(): keys = lax.all_gather(keys, 'head', axis=1, tiled=True)  25.4 us
    all_to_all x1, waiting for transfers between devices, body(): lax.all_to_all(found, 'seq', split_axis=0, concat_axis=0, tiled=True)  25.3 us
    dot_general x1, matrix products, body(): jnp.dot(normed, q_up, preferred_element_type=jnp.float32)  13 us
    pallas_call x1, Pallas kernels, absorbed_query(): pl.pallas_call(absorb_kernel, grid=(group // step,), in_specs=[pl.BlockSp...  9.76 us
    all_gather x1, blocking collectives, body(): lax.all_gather(q_low, 'head', axis=1, tiled=True)  8.71 us
    all_to_all x1, starting transfers between devices, body(): lax.all_to_all(requests, 'seq', split_axis=0, concat_axis=0, tiled=True)  7.31 us
    all_gather x1, blocking collectives, body(): lax.all_gather(q_gain, 'head', axis=0, tiled=True)  5.16 us
  transfers between devices with their start and end apart: 3, of which 3 were waited for; matrix products, arithmetic and copies ran while one was open for 9% of the time, Pallas kernels for 5%

commit v1 on v0

v1 whole, which is shorter than its diff:
```python
import functools

import jax
import jax.numpy as jnp
from jax import lax
from jax.experimental import pallas as pl
from jax.experimental.pallas import tpu as pltpu
from jax.sharding import PartitionSpec as P

NOPE = 128
ROPE = 64
LATENT = 512
VDIM = 128
TILE = 128
TOPT = 16
QBLK = 128
LANES = 128
SUBLANES = 16
LOG2E = 1.4426950408889634
MESH = pl.DeviceIdType.MESH


def rotary_tables(positions):
    half = ROPE // 2
    freq = jnp.power(
        jnp.float32(10000.0), -(2.0 * jnp.arange(half, dtype=jnp.float32)) / ROPE
    )
    angle = positions.astype(jnp.float32)[:, None] * freq[None, :]
    cosine, sine = jnp.cos(angle), jnp.sin(angle)
    return (
        jnp.concatenate([cosine, cosine], axis=-1),
        jnp.concatenate([-sine, sine], axis=-1),
    )


def request_kernel(n, ask_ref, serve_ref, send, recv):
    me = lax.axis_index("seq")
    barrier = pltpu.get_barrier_semaphore()
    for shift in range(1, n):
        pl.semaphore_signal(
            barrier, inc=1, device_id={"seq": lax.rem(me + shift, n)}, device_id_type=MESH
        )
    pl.semaphore_wait(barrier, n - 1)
    copies = []
    for shift in range(1, n):
        peer = lax.rem(me + shift, n)
        copies.append(
            pltpu.make_async_remote_copy(
                src_ref=ask_ref.at[peer],
                dst_ref=serve_ref.at[me],
                send_sem=send.at[shift],
                recv_sem=recv.at[shift],
                device_id={"seq": peer},
                device_id_type=MESH,
            )
        )
        copies[-1].start()
    serve_ref[me] = ask_ref[me]
    for copy in copies:
        copy.wait()


def exchange_requests(ask):
    n = ask.shape[0]
    return pl.pallas_call(
        functools.partial(request_kernel, n),
        out_shape=jax.ShapeDtypeStruct(ask.shape, ask.dtype),
        in_specs=[pl.BlockSpec(memory_space=pltpu.VMEM)],
        out_specs=pl.BlockSpec(memory_space=pltpu.VMEM),
        scratch_shapes=[pltpu.SemaphoreType.DMA((n,)), pltpu.SemaphoreType.DMA((n,))],
        compiler_params=pltpu.CompilerParams(collective_id=0, has_side_effects=True),
        name="requests",
    )(ask)


def main_kernel(
    dims,
    early_ref,
    late_ref,
    found_ref,
    low_ref,
    up_hbm,
    key_hbm,
    value_hbm,
    cos_ref,
    sin_ref,
    out_ref,
    land_a,
    land_b,
    lows,
    normed,
    up_buf,
    key_buf,
    value_buf,
    full_q,
    turned,
    values,
    part,
    part_top,
    part_sum,
    send_a,
    recv_a,
    send_x,
    recv_x,
    send_p,
    recv_p,
    low_send,
    low_recv,
    weight_sem,
    up_sem,
):
    n, lanes_x, half, grain, rows, heads = dims
    subs = half // grain
    me = lax.axis_index("seq")
    place = lax.axis_index("head")
    column, core = place // 2, lax.rem(place, 2)
    mate = column * 2 + (1 - core)
    lands = (land_a, land_b)
    blocks = rows // QBLK

    def beside(step):
        return lax.rem(column + step, lanes_x) * 2 + core

    def behind(step):
        return lax.rem(column + lanes_x - step, lanes_x) * 2 + core

    barrier = pltpu.get_barrier_semaphore()
    for shift in range(1, n):
        pl.semaphore_signal(
            barrier, inc=1, device_id={"seq": lax.rem(me + shift, n)}, device_id_type=MESH
        )
    for step in range(1, lanes_x):
        pl.semaphore_signal(barrier, inc=1, device_id={"head": beside(step)}, device_id_type=MESH)
    pl.semaphore_signal(barrier, inc=1, device_id={"head": mate}, device_id_type=MESH)
    pl.semaphore_wait(barrier, n - 1 + lanes_x)

    def low_copy(src, slot, step, peer, index):
        return pltpu.make_async_remote_copy(
            src_ref=src,
            dst_ref=lows.at[slot],
            send_sem=low_send.at[index, step],
            recv_sem=low_recv.at[index, step],
            device_id={"head": peer},
            device_id_type=MESH,
        )

    low_own = pltpu.make_async_copy(low_ref, lows.at[place], low_recv.at[0, 0])
    low_own.start()
    for step in range(1, lanes_x):
        low_copy(low_ref, place, step, beside(step), 0).start()
    low_copy(low_ref, place, 0, mate, 1).start()

    def seq_copy(part_at, sub, shift):
        peer = lax.rem(me + shift, n)
        return pltpu.make_async_remote_copy(
            src_ref=found_ref.at[peer, pl.ds(part_at * half + sub * grain, grain)],
            dst_ref=lands[part_at].at[pl.ds(me * half + sub * grain, grain), place],
            send_sem=send_a.at[part_at, sub, shift],
            recv_sem=recv_a.at[part_at, sub, shift],
            device_id={"seq": peer},
            device_id_type=MESH,
        )

    def share(part_at, sub, shift, column_at):
        source = lax.rem(me + n - shift, n)
        return lands[part_at].at[pl.ds(source * half + sub * grain, grain), column_at]

    def side_copy(part_at, sub, shift, step):
        ref = share(part_at, sub, shift, place)
        return pltpu.make_async_remote_copy(
            src_ref=ref,
            dst_ref=ref,
            send_sem=send_x.at[part_at, sub, shift, step],
            recv_sem=recv_x.at[part_at, sub, shift, step],
            device_id={"head": beside(step)},
            device_id_type=MESH,
        )

    def mate_copy(part_at, sub, shift, step):
        ref = share(part_at, sub, shift, behind(step))
        return pltpu.make_async_remote_copy(
            src_ref=ref,
            dst_ref=ref,
            send_sem=send_p.at[part_at, sub, shift, step],
            recv_sem=recv_p.at[part_at, sub, shift, step],
            device_id={"head": mate},
            device_id_type=MESH,
        )

    def self_copy(part_at, sub):
        return pltpu.make_async_copy(
            found_ref.at[me, pl.ds(part_at * half + sub * grain, grain)],
            share(part_at, sub, 0, place),
            recv_a.at[part_at, sub, 0],
        )

    for part_at in range(2):
        for sub in range(subs):
            self_copy(part_at, sub).start()
            for shift in range(1, n):
                seq_copy(part_at, sub, shift).start()

    key_copy = pltpu.make_async_copy(key_hbm, key_buf, weight_sem.at[0])
    value_copy = pltpu.make_async_copy(value_hbm, value_buf, weight_sem.at[1])
    key_copy.start()
    value_copy.start()

    pair_width = 2 * (NOPE + ROPE)
    pairs = heads // 2

    def up_copy(index, slot):
        return pltpu.make_async_copy(
            up_hbm.at[:, pl.ds(pl.multiple_of(index * pair_width, LANES), pair_width)],
            up_buf.at[slot],
            up_sem.at[slot],
        )

    up_copy(0, 0).start()

    def pass_on(part_at, sub, shift):
        for step in range(1, lanes_x):
            side_copy(part_at, sub, shift, step).start()
        mate_copy(part_at, sub, shift, 0).start()

    def relay(part_at, sub, shift):
        for step in range(1, lanes_x):
            side_copy(part_at, sub, shift, step).wait_recv()
            mate_copy(part_at, sub, shift, step).start()

    items = subs * (n - 1)
    lag = 3

    def serve(part_at, item):
        sub, shift = item // (n - 1), 1 + lax.rem(item, n - 1)
        seq_copy(part_at, sub, shift).wait_recv()
        pass_on(part_at, sub, shift)

    def serve_relay(part_at, item):
        relay(part_at, item // (n - 1), 1 + lax.rem(item, n - 1))

    def advance(part_at, item):
        @pl.when(item < items)
        def _():
            serve(part_at, item)

        @pl.when((item >= lag) & (item < items + lag))
        def _():
            serve_relay(part_at, item - lag)

    for part_at in range(2):
        for sub in range(subs):
            self_copy(part_at, sub).wait()
            pass_on(part_at, sub, 0)

    low_own.wait()
    for step in range(1, lanes_x):
        low_copy(low_ref, place, step, beside(step), 0).wait_recv()
        slot = behind(step)
        low_copy(lows.at[slot], slot, step, mate, 1).start()
    for part_at in range(2):
        for sub in range(subs):
            relay(part_at, sub, 0)
    for step in range(lanes_x):
        low_copy(low_ref, place, step, mate, 1).wait_recv()

    shares = 2 * lanes_x
    wide = low_ref.shape[1]
    strip = 64

    @pl.loop(0, rows // strip)
    def _(index):
        span = pl.ds(pl.multiple_of(index * strip, strip), strip)
        pieces = [lows[slot, span, :].astype(jnp.float32) for slot in range(shares)]
        power = sum(jnp.sum(piece * piece, axis=-1, keepdims=True) for piece in pieces)
        inverse = lax.rsqrt(power / (wide * shares) + 1e-06)
        scaled = [
            piece * inverse * lows[slot, rows : rows + SUBLANES, :][:1].astype(jnp.float32)
            for slot, piece in enumerate(pieces)
        ]
        normed[span, :] = jnp.concatenate(scaled, axis=-1).astype(jnp.bfloat16)

    key_copy.wait()
    rope_half = ROPE // 2

    @pl.loop(0, pairs)
    def _(index):
        slot = lax.rem(index, 2)

        @pl.when(index + 1 < pairs)
        def _():
            up_copy(index + 1, lax.rem(index + 1, 2)).start()

        up_copy(index, slot).wait()
        query = jnp.dot(normed[...], up_buf[slot], preferred_element_type=jnp.float32).astype(
            jnp.bfloat16
        )
        cosine, sine = cos_ref[...], sin_ref[...]
        for head in range(2):
            start = head * (NOPE + ROPE)
            nope = query[:, start : start + NOPE]
            rope = query[:, start + NOPE : start + NOPE + ROPE].astype(jnp.float32)
            swapped = jnp.concatenate([rope[:, rope_half:], rope[:, :rope_half]], axis=-1)
            rotated = rope * cosine + swapped * sine
            full_q[index * 2 + head, :, :LATENT] = jnp.dot(
                nope, key_buf[index * 2 + head], preferred_element_type=jnp.float32
            ).astype(jnp.bfloat16)
            full_q[index * 2 + head, :, LATENT:] = jnp.concatenate(
                [rotated, jnp.zeros((rows, LANES - ROPE), jnp.float32)], axis=-1
            ).astype(jnp.bfloat16)

        @pl.when(lax.rem(index, 2) == 1)
        def _():
            advance(0, index // 2)

    width = LATENT + ROPE
    turned[width:, :] = jnp.zeros((turned.shape[0] - width, turned.shape[1]), turned.dtype)

    @pl.loop(pairs // 2, items + lag)
    def _(item):
        advance(0, item)

    def wait_mate(part_at):
        for sub in range(subs):
            @pl.loop(0, n)
            def _(shift):
                for step in range(lanes_x):
                    mate_copy(part_at, sub, shift, step).wait_recv()

    wait_mate(0)
    value_copy.wait()

    scale = float(NOPE + ROPE) ** (-0.5) * LOG2E
    step_heads = 4
    groups = heads // step_heads
    per = -(-(items + lag) // (2 * groups))
    count = TOPT // 2

    def place_tile(at, tile):
        tile = tile.reshape(width, TILE)
        turned[:width, at * TILE : (at + 1) * TILE] = tile
        values[at * TILE : (at + 1) * TILE, :] = tile[:LATENT].T

    def fill_early(block):
        for at in range(count):
            place_tile(at, land_a[early_ref[block * count + at]])

    def fill_late(block):
        for at in range(count):
            base = 3 * (block * count + at)
            first = land_a[late_ref[base]]
            second = land_b[late_ref[base + 1]]
            flag = jnp.full(first.shape, late_ref[base + 2], jnp.int32) > 0
            place_tile(at, jnp.where(flag, first, second))

    def attend(block, group, last):
        span = slice(block * QBLK, (block + 1) * QBLK)
        scores = []
        for at in range(0, step_heads, 2):
            queries = full_q[pl.ds(group * step_heads + at, 2), span].reshape(
                2 * QBLK, full_q.shape[2]
            )
            scores.append(jnp.dot(queries, turned[...], preferred_element_type=jnp.float32))
        for at in range(0, step_heads, 2):
            score = scores[at // 2]
            top = jnp.max(score, axis=-1, keepdims=True)
            weights = jnp.exp2((score - top) * scale)
            total = jnp.sum(weights, axis=-1, keepdims=True)
            mixed = jnp.dot(
                weights.astype(jnp.bfloat16), values[...], preferred_element_type=jnp.float32
            )
            mixed = (mixed / total).astype(jnp.bfloat16)
            for sub_head in range(2):
                head = group * step_heads + at + sub_head
                lines = slice(sub_head * QBLK, (sub_head + 1) * QBLK)
                result = jnp.dot(
                    mixed[lines], value_buf[head], preferred_element_type=jnp.float32
                )
                if not last:
                    part[block, head] = result
                    part_top[block, head] = top[lines]
                    part_sum[block, head] = total[lines]
                else:
                    old_top, old_sum = part_top[block, head], part_sum[block, head]
                    peak = jnp.maximum(old_top, top[lines])
                    old = old_sum * jnp.exp2((old_top - peak) * scale)
                    new = total[lines] * jnp.exp2((top[lines] - peak) * scale)
                    merged = (part[block, head] * old + result * new) / (old + new)
                    out_ref[
                        span, pl.ds(pl.multiple_of(head * VDIM, VDIM), VDIM)
                    ] = merged.astype(jnp.bfloat16)

    for block in range(blocks):
        fill_early(block)

        @pl.loop(0, groups)
        def _(group):
            attend(block, group, False)
            for extra in range(per):
                advance(1, (block * groups + group) * per + extra)

    wait_mate(1)
    for block in range(blocks):
        fill_late(block)

        @pl.loop(0, groups)
        def _(group):
            attend(block, group, True)

    for part_at in range(2):
        for sub in range(subs):
            @pl.loop(1, n)
            def _(shift):
                seq_copy(part_at, sub, shift).wait_send()

            @pl.loop(0, n)
            def _(shift):
                for step in range(1, lanes_x):
                    side_copy(part_at, sub, shift, step).wait_send()
                for step in range(lanes_x):
                    mate_copy(part_at, sub, shift, step).wait_send()
    for step in range(1, lanes_x):
        low_copy(low_ref, place, step, beside(step), 0).wait_send()
    for step in range(lanes_x):
        low_copy(low_ref, place, step, mate, 1).wait_send()


def exchange_and_attend(early, late, found, low, q_up, key_absorb, value_absorb, cosine, sine):
    n, cap, part_width, tile = found.shape
    head_count = lax.axis_size("head")
    half = cap // 2
    grain = max(1, half // 2)
    subs = half // grain
    lanes_x = head_count // 2
    heads = key_absorb.shape[0]
    rows = low.shape[0] - SUBLANES
    blocks = rows // QBLK
    depth = q_up.shape[0]
    padded = LATENT + LANES
    count = TOPT // 2 * TILE
    any_spec = pl.BlockSpec(memory_space=pl.ANY)
    vmem_spec = pl.BlockSpec(memory_space=pltpu.VMEM)
    smem_spec = pl.BlockSpec(memory_space=pltpu.SMEM)
    dma = pltpu.SemaphoreType.DMA
    land = pltpu.VMEM((n * half, head_count, part_width, tile), jnp.bfloat16)
    dims = (n, lanes_x, half, grain, rows, heads)
    return pl.pallas_call(
        functools.partial(main_kernel, dims),
        out_shape=jax.ShapeDtypeStruct((rows, heads * VDIM), jnp.bfloat16),
        in_specs=[smem_spec, smem_spec] + [any_spec] * 5 + [vmem_spec] * 2,
        out_specs=vmem_spec,
        scratch_shapes=[
            land,
            land,
            pltpu.VMEM((head_count,) + low.shape, jnp.bfloat16),
            pltpu.VMEM((rows, depth), jnp.bfloat16),
            pltpu.VMEM((2, depth, 2 * (NOPE + ROPE)), jnp.bfloat16),
            pltpu.VMEM(key_absorb.shape, jnp.bfloat16),
            pltpu.VMEM(value_absorb.shape, jnp.bfloat16),
            pltpu.VMEM((heads, rows, padded), jnp.bfloat16),
            pltpu.VMEM((padded, count), jnp.bfloat16),
            pltpu.VMEM((count, LATENT), jnp.bfloat16),
            pltpu.VMEM((blocks, heads, QBLK, VDIM), jnp.float32),
            pltpu.VMEM((blocks, heads, QBLK, 1), jnp.float32),
            pltpu.VMEM((blocks, heads, QBLK, 1), jnp.float32),
            dma((2, subs, n)),
            dma((2, subs, n)),
            dma((2, subs, n, lanes_x)),
            dma((2, subs, n, lanes_x)),
            dma((2, subs, n, lanes_x)),
            dma((2, subs, n, lanes_x)),
            dma((2, lanes_x)),
            dma((2, lanes_x)),
            dma((2,)),
            dma((2,)),
        ],
        compiler_params=pltpu.CompilerParams(
            collective_id=1, has_side_effects=True, vmem_limit_bytes=62 * 1024 * 1024
        ),
        cost_estimate=pl.CostEstimate(
            flops=2 * rows * heads * TOPT * TILE * (padded + LATENT),
            bytes_accessed=2 * (q_up.size + 2 * key_absorb.size),
            transcendentals=rows * heads * TOPT * TILE,
        ),
        name="exchange_attend",
    )(early, late, found, low, q_up, key_absorb, value_absorb, cosine, sine)


def slot_plan(picks, tiles_dev, seq_count, cap):
    total = picks.shape[0]
    half = cap // 2
    order = jnp.arange(total, dtype=jnp.int32)
    block = order // TOPT
    owner = picks // tiles_dev
    same = picks[:, None] == picks[None, :]
    first = jnp.min(jnp.where(same, order[None, :], total), axis=1)
    fresh = first == order
    shared = jnp.sum(same.astype(jnp.int32), axis=1) > 1
    kind = jnp.where(shared, 2, block)
    owned = owner[:, None] == jnp.arange(seq_count, dtype=jnp.int32)[None, :]

    def tally(which):
        hit = owned & (fresh & (kind == which))[:, None]
        return jnp.sum(hit.astype(jnp.int32), axis=0)

    tallies = [tally(which) for which in range(3)]
    odd_a, odd_b, odd_c = [size % 2 for size in tallies]
    split = odd_a * odd_b * (1 - odd_c)
    seqs = jnp.arange(seq_count, dtype=jnp.int32)
    turn = jnp.sum(jnp.where(seqs[None, :] < seqs[:, None], split[None, :], 0), axis=1) % 2
    up_a = jnp.where(odd_c == 1, odd_b, jnp.where(odd_b == 1, turn, 1))
    up_b = jnp.where(odd_c == 1, 0, jnp.where(odd_a == 1, 1 - turn, 1))
    early_a = tallies[0] // 2 + odd_a * up_a
    early_b = tallies[1] // 2 + odd_b * up_b
    early_c = (tallies[2] + 1) // 2
    rest_a, rest_b = tallies[0] - early_a, tallies[1] - early_b
    zero = jnp.zeros_like(early_a)
    quotas = jnp.stack([early_a, early_b, early_c])
    starts = jnp.stack([zero, early_a, early_a + early_b])
    rests = jnp.stack([zero, rest_a, rest_a + rest_b])
    chosen = owned[:, None, :] & (kind[:, None] == jnp.arange(3)[None, :])[:, :, None]

    def look(table):
        return jnp.sum(jnp.where(chosen, table[None], 0), axis=(1, 2))

    quota, start, rest = look(quotas), look(starts), look(rests)
    before = (
        (owner[:, None] == owner[None, :])
        & (kind[:, None] == kind[None, :])
        & fresh[None, :]
        & (order[None, :] < first[:, None])
    )
    index = jnp.sum(before.astype(jnp.int32), axis=1)
    early = index < quota
    spot = jnp.where(early, start + index, rest + index - quota)
    slot = owner * cap + jnp.where(early, spot, half + spot)
    hit = (slot[:, None] == jnp.arange(seq_count * cap, dtype=jnp.int32)[None, :]) & fresh[:, None]
    ask = jnp.sum(jnp.where(hit, (picks % tiles_dev)[:, None], 0), axis=0)
    land = owner * half + spot
    earlier = (block[:, None] == block[None, :]) & (order[None, :] < order[:, None])
    seen = jnp.sum((earlier & early[None, :]).astype(jnp.int32), axis=1)
    now = early & (seen < TOPT // 2)
    position = jnp.sum((earlier & (now[None, :] == now[:, None])).astype(jnp.int32), axis=1)
    position = block * (TOPT // 2) + position
    places = jnp.arange(total // 2, dtype=jnp.int32)
    at = position[:, None] == places[None, :]
    first_table = jnp.sum(jnp.where(at & now[:, None], land[:, None], 0), axis=0)
    later = at & ~now[:, None]
    fields = jnp.stack(
        [jnp.where(early, land, 0), jnp.where(early, 0, land), early.astype(jnp.int32)], axis=1
    )
    second_table = jnp.sum(jnp.where(later[:, :, None], fields[:, None, :], 0), axis=0)
    return ask.reshape(seq_count, cap), first_table, second_table.reshape(-1)


def body(q_low, q_gain, q_up, key_absorb, value_absorb, latent_cache, tile_picks):
    rows = q_low.shape[0]
    width = latent_cache.shape[1]
    seq_count = lax.axis_size("seq")
    tiles_dev = latent_cache.shape[0] // TILE
    picks = tile_picks.reshape(-1)
    count = picks.shape[0]
    cap = max(2, 2 * count // seq_count)
    ask, early, late = slot_plan(picks, tiles_dev, seq_count, cap)
    ask = jnp.pad(ask, ((0, 0), (0, LANES - cap))).reshape(seq_count, 1, LANES)
    serve = exchange_requests(ask).reshape(seq_count, LANES)[:, :cap]
    share = width // lax.axis_size("head")
    columns = lax.dynamic_slice_in_dim(latent_cache, lax.axis_index("head") * share, share, 1)
    cache_tiles = columns.T.reshape(share, tiles_dev, TILE).transpose(1, 0, 2)
    found = jnp.take(cache_tiles, serve, axis=0, mode="clip")
    low = jnp.concatenate(
        [q_low, jnp.broadcast_to(q_gain[None, :], (SUBLANES, q_gain.shape[0]))], axis=0
    )
    context = latent_cache.shape[0] * seq_count
    positions = context + lax.axis_index("seq") * rows + jnp.arange(rows, dtype=jnp.int32)
    cosine, sine = rotary_tables(positions)
    return exchange_and_attend(
        early, late, found, low, q_up, key_absorb, value_absorb, cosine, sine
    )


def solution(mesh):
    in_specs = (
        P("seq", "head"),
        P("head"),
        P(None, "head"),
        P("head", None, None),
        P("head", None, None),
        P("seq", None),
        P("seq", None),
    )
    out_specs = P("seq", "head")
    return jax.shard_map(body, mesh=mesh, in_specs=in_specs, out_specs=out_specs, check_vma=False)
```

time: 189 us -> 151 us (0.80); the launches traced: 189 us -> 148 us
  Pallas kernels: 71 us -> 133 us
  waiting for transfers between devices: 55.1 us -> 0 us
  blocking collectives: 13.9 us -> 0 us
  between operations: 13.5 us -> 0.18 us
  matrix products: 13 us -> 0 us
  starting transfers between devices: 11.1 us -> 0 us
  local copies, waits for them, and re-layouts: 8.19 us -> 10.5 us
    pallas_call x2, Pallas kernels: 71 us -> 133 us  [the longest x1 124 us: exchange_and_attend(): pl.pallas_call(functools.partial(main_kernel, dims), out_shape=jax.ShapeD...]
    all_to_all x2 -> x0, waiting for transfers between devices: 29.6 us -> none  [the longest x1 25.3 us: body(): lax.all_to_all(found, 'seq', split_axis=0, concat_axis=0, tiled=True)]
    all_gather x1 -> x0, waiting for transfers between devices: 25.4 us -> none  [body(): keys = lax.all_gather(keys, 'head', axis=1, tiled=True)]
    all_gather x2 -> x0, blocking collectives: 13.9 us -> none  [the longest x1 8.71 us: body(): lax.all_gather(q_low, 'head', axis=1, tiled=True)]
    dot_general x1 -> x0, matrix products: 13 us -> none  [body(): jnp.dot(normed, q_up, preferred_element_type=jnp.float32)]
    all_to_all x2 -> x0, starting transfers between devices: 11.1 us -> none  [the longest x1 7.31 us: body(): lax.all_to_all(requests, 'seq', split_axis=0, concat_axis=0, tiled=True)]
    unnamed x7, local copies, waits for them, and re-layouts: 0.02 us -> 3.15 us
    gather x2 -> x1, local copies, waits for them, and re-layouts: 3.98 us -> 2.27 us  [body(): found = jnp.take(cache_tiles, serve, axis=0, mode='clip')]
  transfers between devices with their start and end apart: 3 -> 0, of which waited for: 3 -> 0; matrix products, arithmetic and copies ran while one was open for 9% -> 0% of each run, Pallas kernels for 5% -> 0%
where the time goes in v1:
time: 151 us; the launch traced here: 148 us
  Pallas kernels  133 us (88%)
  local copies, waits for them, and re-layouts  10.5 us (7%)
  other arithmetic  4.21 us (3%)
    pallas_call x1, Pallas kernels, exchange_and_attend(): pl.pallas_call(functools.partial(main_kernel, dims), out_shape=jax.ShapeD...  124 us
    pallas_call x1, Pallas kernels, exchange_requests(): pl.pallas_call(functools.partial(request_kernel, n), out_shape=jax.ShapeD...  9.59 us
    unnamed x7, local copies, waits for them, and re-layouts  3.15 us

profile of v1, /device:TPU:0, one launch (start us, length us, event | category | flops | bytes accessed | tf_op | source)
XLA Modules:
  0.0 148.1 jit_solution(15938977824830550753)
XLA Ops:
  0.0 0.8 reshape.856
  0.8 0.2 fusion.1
  1.0 0.1 convert_reduce_fusion.5
  1.1 0.1 select_reduce_fusion.3
  1.4 0.1 fusion.7
  1.5 0.2 convert_reduce_fusion.2
  1.7 0.1 select_reduce_fusion.1
  1.8 0.1 reshape.860
  1.8 0.6 pad.4
  2.5 9.6 %requests.1 = s32[8,1,128]{2,1,0:T(1,128)} custom-call(s32[8,1,128]{2,1,0:T(1,128)} %bitcast.119), custom_call_target="tpu_custom_call" | custom-call | tf_op jit(solution)/shard_map/requests/pallas_call | solution.py:65
  12.1 0.8 reshape.865
  12.8 2.1 %bitcast_bitcast_fusion = bf16[64,144,128]{2,1,0:T(8,128)(2,1)S(1)} fusion(bf16[8192,576]{0,1:T(8,128)(2,1)} %param.12, s32[]{:T(128)S(6)} %select_n.469), kind=kLoop, calls=%fused_computation.1 | loop fusion | bytes 4718596 | tf_op jit(solution)/shard_map/transpose | solution.py:568
  14.9 0.0 copy-start.2
  14.9 0.0 copy-start.1
  14.9 0.0 copy-start
  14.9 2.3 %gather_fusion = bf16[64,144,128]{2,1,0:T(8,128)(2,1)} fusion(bf16[64,144,128]{2,1,0:T(8,128)(2,1)S(1)} %bitcast_bitcast_fusion, s32[1024]{0:T(1024)S(1)} %pad_clamp_fusion), kind=kCustom, calls=%fused_computation | custom fusion | bytes 4718848 | tf_op jit(solution)/shard_map/jit(_take)/gather | solution.py:569
  17.2 0.2 convert_reduce_fusion.1
  17.4 0.2 convert_reduce_fusion
  17.6 0.0 copy-done.2
  17.6 0.1 reshape.857
  17.8 0.1 select_reduce_fusion
  17.9 0.1 copy.14
  18.0 0.7 reshape.858.late_ref
  18.7 0.6 select_reduce_fusion.2.early_ref
  19.3 0.5 fusion
  19.8 0.8 pad_maximum_fusion.1
  20.7 0.0 copy-done.1
  20.7 0.0 copy-done
  20.7 0.7 pad_maximum_fusion.low_ref
  21.4 123.5 %exchange_attend.1 = bf16[256,4096]{1,0:T(8,128)(2,1)} custom-call(s32[16]{0:T(128)} %select_reduce_fusion.2.early_ref, s32[48]{0:T(128)} %reshape.858.late_ref, bf16[8,8,144,128]{3,2,1,0:T(8,128)(2,1)} %bitcast.118, bf16[272,384]{1,0:T(8,128)(2,1)} %pad_maximum_fusion.low_ref, bf16[1536,6144]{1,0:T(8,128)(2,1)} %up_hbm.1, bf16[32,128,512]{2,1,0:T(8,128)(2,1)} %key_hbm.1, ...), custom_call_target="tpu_custom_call" | custom-call | flops 38654705664 | bytes 27262976 | tf_op jit(solution)/shard_map/exchange_attend/pallas_call | solution.py:446
  144.9 3.1 %copy.20 = bf16[256,4096]{1,0:T(8,128)(2,1)} copy(bf16[256,4096]{1,0:T(8,128)(2,1)} %exchange_attend.1) | data formatting | bytes 4194304
  (23 shorter events, 0.2 us)
Async XLA Ops:
  14.9 2.7 %copy-start.2 = (s32[2,16]{1,0:T(2,128)S(1)}, s32[2,16]{1,0:T(2,128)}, u32[]{:S(2)}) copy-start(s32[2,16]{1,0:T(2,128)} %param.13) | copy-start | bytes 388
  14.9 5.8 %copy-start.1 = (bf16[384]{0:T(512)(128)(2,1)S(1)}, bf16[384]{0:T(512)(128)(2,1)}, u32[]{:S(2)}) copy-start(bf16[384]{0:T(512)(128)(2,1)} %param.8) | copy-start | bytes 2308
  14.9 5.8 %copy-start = (bf16[256,384]{1,0:T(8,128)(2,1)S(1)}, bf16[256,384]{1,0:T(8,128)(2,1)}, u32[]{:S(2)}) copy-start(bf16[256,384]{1,0:T(8,128)(2,1)} %param.7) | copy-start | bytes 589828
